TPU v7x, 256 devices: a whole 4x4x8 slice. The times are simulated.
256 devices in a mesh: outer: 32 (over z, y), inner: 8 (over x, core).
Axes of the slice: x: 4, y: 4, z: 8, core: 2. Of those that a mesh axis runs over, the one named last changes fastest.
Arguments:
- w_one: float32 [32, 8, 4, 128, 512], P('outer', 'inner')
- w_two: float32 [32, 8, 4, 512, 128], P('outer', 'inner')
- inputs: bfloat16 [32, 8, 16, 64, 128], P('outer', 'inner')
- targets: bfloat16 [32, 8, 16, 64, 128], P('outer', 'inner')
- mix_self: float32 [32, 8, 16], P('outer', 'inner')
Outputs:
- output 1: float32 [32, 8, 4, 128, 512], P('outer', 'inner')
- output 2: float32 [32, 8, 4, 512, 128], P('outer', 'inner')
All inputs are finite; a program needn't handle non-finite values.
Results may differ from a plain program's by a relative error of at most 0.00351111.
Values are sent between devices in bfloat16 or wider.
A program may use at most 768 MiB of HBM per device.

v0:
```python
import jax
import jax.numpy as jnp
from jax import lax
from jax.sharding import PartitionSpec as P

RMS_EPS = 1e-6
RATE_BASE = 1.5


def replica_grads(one_bf, two_bf, inputs, targets):
    n_layers = one_bf.shape[0]
    batch_rows, feat_width = inputs.shape
    hidden = inputs
    saved_acts = []
    for layer_idx in range(n_layers):
        hid_f = hidden.astype(jnp.float32)
        inv_rms = lax.rsqrt(jnp.mean(hid_f * hid_f, axis=-1, keepdims=True) + RMS_EPS)
        normed = (hid_f * inv_rms).astype(jnp.bfloat16)
        pre_act = jnp.dot(normed, one_bf[layer_idx], preferred_element_type=jnp.float32)
        act_f, gelu_back = jax.vjp(jax.nn.gelu, pre_act)
        act_bf = act_f.astype(jnp.bfloat16)
        out_add = jnp.dot(act_bf, two_bf[layer_idx], preferred_element_type=jnp.float32)
        saved_acts.append((hid_f, inv_rms, normed, act_bf, gelu_back))
        hidden = (hid_f + out_add).astype(jnp.bfloat16)
    d_hid = (2.0 / (batch_rows * feat_width)) * (hidden.astype(jnp.float32) - targets.astype(jnp.float32))
    grads_one = [None] * n_layers
    grads_two = [None] * n_layers
    row_dims = (((0,), (0,)), ((), ()))
    feat_dims = (((1,), (1,)), ((), ()))
    for layer_idx in reversed(range(n_layers)):
        hid_f, inv_rms, normed, act_bf, gelu_back = saved_acts[layer_idx]
        d_out = d_hid.astype(jnp.bfloat16)
        grads_two[layer_idx] = lax.dot_general(act_bf, d_out, row_dims, preferred_element_type=jnp.float32)
        d_act = lax.dot_general(d_out, two_bf[layer_idx], feat_dims, preferred_element_type=jnp.float32)
        d_pre = gelu_back(d_act)[0].astype(jnp.bfloat16)
        grads_one[layer_idx] = lax.dot_general(normed, d_pre, row_dims, preferred_element_type=jnp.float32)
        if layer_idx > 0:
            d_norm = lax.dot_general(d_pre, one_bf[layer_idx], feat_dims, preferred_element_type=jnp.float32)
            d_hid = d_hid + inv_rms * d_norm - (inv_rms * inv_rms * inv_rms) * hid_f * jnp.mean(d_norm * hid_f, axis=-1, keepdims=True)
    return jnp.stack(grads_one), jnp.stack(grads_two)


def solution(mesh):
    n_dev = mesh.shape['outer'] * mesh.shape['inner']
    log_g = n_dev.bit_length() - 1
    replica_spec = P('outer', 'inner')

    def device_run(w_one, w_two, inputs, targets, mix_self):
        w_one = w_one[0, 0]
        w_two = w_two[0, 0]
        learn_rate = RATE_BASE / w_one.shape[0]
        for step_idx in range(inputs.shape[2]):
            one_bf = w_one.astype(jnp.bfloat16)
            two_bf = w_two.astype(jnp.bfloat16)
            grad_one, grad_two = replica_grads(one_bf, two_bf, inputs[0, 0, step_idx], targets[0, 0, step_idx])
            peer_shift = 2 ** (step_idx % log_g)
            send_pairs = [(source, (source + peer_shift) % n_dev) for source in range(n_dev)]
            peer_one = lax.ppermute(one_bf, ('outer', 'inner'), send_pairs)
            peer_two = lax.ppermute(two_bf, ('outer', 'inner'), send_pairs)
            self_weight = mix_self[0, 0, step_idx]
            w_one = self_weight * w_one + (1.0 - self_weight) * peer_one.astype(jnp.float32) - learn_rate * grad_one
            w_two = self_weight * w_two + (1.0 - self_weight) * peer_two.astype(jnp.float32) - learn_rate * grad_two
        return w_one[None, None], w_two[None, None]

    return jax.shard_map(device_run, mesh=mesh, in_specs=(replica_spec,) * 5, out_specs=(replica_spec, replica_spec), check_vma=False)
```

profile of v0, /device:TPU:54, one launch (start us, length us, event | category | flops | bytes accessed | tf_op | source)
XLA Modules:
  0.0 688.0 jit_solution(13234289374719641746)
XLA Ops:
  41.8 2.8 fusion.1328
  69.2 4.7 fusion.1354
  76.2 3.7 fusion.1356
  97.8 2.5 collective-permute-start.3
  104.9 2.9 fusion.1326
  109.4 3.2 collective-permute-done.3
  112.7 2.8 fusion.1327
  134.7 4.5 collective-permute-start.5
  145.1 4.4 fusion.1350
  149.7 3.7 fusion.1352
  171.2 5.2 collective-permute-start.7
  181.0 2.8 fusion.1324
  183.9 7.8 %collective-permute-start.12 = (bf16[4,512,128]{2,1,0:T(8,128)(2,1)}, bf16[4,512,128]{2,1,0:T(8,128)(2,1)}, u32[]{:S(2)}, u32[]{:S(2)}) collective-permute-start(bf16[4,512,128]{2,1,0:T(8,128)(2,1)} %fusion.1324), channel_id=1, source_target_pairs={{0,32},{1,33},{2,34},{3,35},{4,36},{5,37},{6,38},{7,39},{8,40},{9,... | collective-permute-start | bytes 1572872 | tf_op jit(solution)/shard_map/ppermute | solution.py:59
  191.7 2.7 fusion.1325
  213.6 4.3 collective-permute-start.9
  223.9 4.4 fusion.1346
  228.3 2.6 collective-permute-start.14
  230.9 3.2 collective-permute-done.9
  234.2 3.6 fusion.1348
  262.8 3.0 fusion.1322
  266.2 32.4 %collective-permute-done.11 = bf16[4,128,512]{2,1,0:T(8,128)(2,1)} collective-permute-done((bf16[4,128,512]{2,1,0:T(8,128)(2,1)}, bf16[4,128,512]{2,1,0:T(8,128)(2,1)}, u32[]{:S(2)}, u32[]{:S(2)}) %collective-permute-start.11) | collective-permute-done | bytes 524320 | tf_op jit(solution)/shard_map/ppermute | solution.py:58
  320.3 4.6 fusion.1342
  324.9 4.2 collective-permute-done.13
  329.2 2.9 fusion.1344
  350.3 3.0 fusion.1320
  353.6 2.7 fusion.1321
  381.7 4.4 fusion.1338
  386.2 4.3 collective-permute-done.17
  390.5 3.7 fusion.1340
  416.9 3.0 fusion.1318
  420.5 12.5 %collective-permute-done.19 = bf16[4,128,512]{2,1,0:T(8,128)(2,1)} collective-permute-done((bf16[4,128,512]{2,1,0:T(8,128)(2,1)}, bf16[4,128,512]{2,1,0:T(8,128)(2,1)}, u32[]{:S(2)}, u32[]{:S(2)}) %collective-permute-start.19) | collective-permute-done | bytes 524320 | tf_op jit(solution)/shard_map/ppermute | solution.py:58
  433.0 2.8 fusion.1319
  461.1 4.5 fusion.1334
  466.5 11.7 %collective-permute-done.21 = bf16[4,128,512]{2,1,0:T(8,128)(2,1)} collective-permute-done((bf16[4,128,512]{2,1,0:T(8,128)(2,1)}, bf16[4,128,512]{2,1,0:T(8,128)(2,1)}, u32[]{:S(2)}, u32[]{:S(2)}) %collective-permute-start.21) | collective-permute-done | bytes 524320 | tf_op jit(solution)/shard_map/ppermute | solution.py:58
  478.2 3.8 fusion.1336
  499.9 5.2 collective-permute-start.23
  509.7 2.9 fusion.1316
  512.6 5.9 collective-permute-start.28
  518.5 2.8 fusion.1317
  540.5 7.9 %collective-permute-start.25 = (bf16[4,128,512]{2,1,0:T(8,128)(2,1)}, bf16[4,128,512]{2,1,0:T(8,128)(2,1)}, u32[]{:S(2)}, u32[]{:S(2)}) collective-permute-start(bf16[4,128,512]{2,1,0:T(8,128)(2,1)} %fusion.1317), channel_id=1, source_target_pairs={{0,32},{1,33},{2,34},{3,35},{4,36},{5,37},{6,38},{7,39},{8,40},{9,... | collective-permute-start | bytes 1572872 | tf_op jit(solution)/shard_map/ppermute | solution.py:58
  554.4 4.5 fusion.1330
  562.2 3.7 fusion.1332
  588.7 2.9 fusion.1314
  591.6 5.7 collective-permute-start.31
  597.3 14.0 %collective-permute-done.27 = bf16[4,128,512]{2,1,0:T(8,128)(2,1)} collective-permute-done((bf16[4,128,512]{2,1,0:T(8,128)(2,1)}, bf16[4,128,512]{2,1,0:T(8,128)(2,1)}, u32[]{:S(2)}, u32[]{:S(2)}) %collective-permute-start.27) | collective-permute-done | bytes 524320 | tf_op jit(solution)/shard_map/ppermute | solution.py:58
  626.7 46.5 %collective-permute-start.29 = (bf16[4,128,512]{2,1,0:T(8,128)(2,1)S(1)}, bf16[4,128,512]{2,1,0:T(8,128)(2,1)}, u32[]{:S(2)}, u32[]{:S(2)}) collective-permute-start(bf16[4,128,512]{2,1,0:T(8,128)(2,1)S(1)} %fusion.1315), channel_id=1, source_target_pairs={{0,128},{1,129},{2,130},{3,131},{4,132},{5,133},{6,134},{7,135},{8... | collective-permute-start | bytes 1572872 | tf_op jit(solution)/shard_map/ppermute | solution.py:58
  679.1 4.5 fusion.193
  683.7 3.8 fusion.191
  (828 shorter events, 387.2 us)
Async XLA Ops:
  2.8 39.0 %collective-permute-start.2 = (bf16[4,512,128]{2,1,0:T(8,128)(2,1)}, bf16[4,512,128]{2,1,0:T(8,128)(2,1)}, u32[]{:S(2)}, u32[]{:S(2)}) collective-permute-start(bf16[4,512,128]{2,1,0:T(8,128)(2,1)} %convert_bitcast_fusion.16), channel_id=1, source_target_pairs={{0,1},{1,2},{2,3},{3,4},{4,5},{5,6},{6,7},{7,8},{8,9},{9,10},{10,1... | collective-permute-start | bytes 1572872 | tf_op jit(solution)/shard_map/ppermute | solution.py:59
  3.7 42.5 %collective-permute-start = (bf16[4,128,512]{2,1,0:T(8,128)(2,1)}, bf16[4,128,512]{2,1,0:T(8,128)(2,1)}, u32[]{:S(2)}, u32[]{:S(2)}) collective-permute-start(bf16[4,128,512]{2,1,0:T(8,128)(2,1)} %convert_bitcast_fusion.17), channel_id=1, source_target_pairs={{0,1},{1,2},{2,3},{3,4},{4,5},{5,6},{6,7},{7,8},{8,9},{9,10},{10,1... | collective-permute-start | bytes 1572872 | tf_op jit(solution)/shard_map/ppermute | solution.py:58
  12.1 29.7 %copy-start.44 = (f32[1,512,128]{2,1,0:T(8,128)}, f32[1,512,128]{2,1,0:T(8,128)S(1)}, u32[]{:S(2)}) copy-start(f32[1,512,128]{2,1,0:T(8,128)S(1)} %convolution_bitcast_fusion.122) | copy-start | bytes 786436
  16.9 25.0 %copy-start.12 = (f32[1,512,128]{2,1,0:T(8,128)}, f32[1,512,128]{2,1,0:T(8,128)S(1)}, u32[]{:S(2)}) copy-start(f32[1,512,128]{2,1,0:T(8,128)S(1)} %convolution_bitcast_fusion.123) | copy-start | bytes 786436
  18.6 27.6 %copy-start.8 = (f32[1,128,512]{2,1,0:T(8,128)}, f32[1,128,512]{2,1,0:T(8,128)S(1)}, u32[]{:S(2)}) copy-start(f32[1,128,512]{2,1,0:T(8,128)S(1)} %convolution_bitcast_fusion.125) | copy-start | bytes 786436
  18.9 27.3 %copy-start.10 = (f32[1,128,512]{2,1,0:T(8,128)}, f32[1,128,512]{2,1,0:T(8,128)S(1)}, u32[]{:S(2)}) copy-start(f32[1,128,512]{2,1,0:T(8,128)S(1)} %convolution_bitcast_fusion.124) | copy-start | bytes 786436
  30.6 17.5 %copy-start.122 = (f32[64]{0:T(128)}, f32[64]{0:T(128)S(1)}, u32[]{:S(2)}) copy-start(f32[64]{0:T(128)S(1)} %add_rsqrt_fusion.59) | copy-start | bytes 772
  44.7 24.5 %collective-permute-start.4 = (bf16[4,512,128]{2,1,0:T(8,128)(2,1)}, bf16[4,512,128]{2,1,0:T(8,128)(2,1)}, u32[]{:S(2)}, u32[]{:S(2)}) collective-permute-start(bf16[4,512,128]{2,1,0:T(8,128)(2,1)} %fusion.1328), channel_id=1, source_target_pairs={{0,2},{1,3},{2,4},{3,5},{4,6},{5,7},{6,8},{7,9},{8,10},{9,11},{10,... | collective-permute-start | bytes 1572872 | tf_op jit(solution)/shard_map/ppermute | solution.py:59
  61.7 14.5 %collective-permute-start.1 = (bf16[4,128,512]{2,1,0:T(8,128)(2,1)S(1)}, bf16[4,128,512]{2,1,0:T(8,128)(2,1)}, u32[]{:S(2)}, u32[]{:S(2)}) collective-permute-start(bf16[4,128,512]{2,1,0:T(8,128)(2,1)S(1)} %fusion.1329), channel_id=1, source_target_pairs={{0,2},{1,3},{2,4},{3,5},{4,6},{5,7},{6,8},{7,9},{8,10},{9,11},{10,... | collective-permute-start | bytes 1572872 | tf_op jit(solution)/shard_map/ppermute | solution.py:58
  73.9 31.0 %collective-permute-start.6 = (bf16[4,512,128]{2,1,0:T(8,128)(2,1)}, bf16[4,512,128]{2,1,0:T(8,128)(2,1)}, u32[]{:S(2)}, u32[]{:S(2)}) collective-permute-start(bf16[4,512,128]{2,1,0:T(8,128)(2,1)} %get-tuple-element.42), channel_id=1, source_target_pairs={{0,4},{1,5},{2,6},{3,7},{4,8},{5,9},{6,10},{7,11},{8,12},{9,13},{1... | collective-permute-start | bytes 1572872 | tf_op jit(solution)/shard_map/ppermute | solution.py:59
  97.8 14.9 %collective-permute-start.3 = (bf16[4,128,512]{2,1,0:T(8,128)(2,1)}, bf16[4,128,512]{2,1,0:T(8,128)(2,1)}, u32[]{:S(2)}, u32[]{:S(2)}) collective-permute-start(bf16[4,128,512]{2,1,0:T(8,128)(2,1)} %get-tuple-element.44), channel_id=1, source_target_pairs={{0,4},{1,5},{2,6},{3,7},{4,8},{5,9},{6,10},{7,11},{8,12},{9,13},{1... | collective-permute-start | bytes 1572872 | tf_op jit(solution)/shard_map/ppermute | solution.py:58
  107.8 37.3 %collective-permute-start.8 = (bf16[4,512,128]{2,1,0:T(8,128)(2,1)}, bf16[4,512,128]{2,1,0:T(8,128)(2,1)}, u32[]{:S(2)}, u32[]{:S(2)}) collective-permute-start(bf16[4,512,128]{2,1,0:T(8,128)(2,1)} %fusion.1326), channel_id=1, source_target_pairs={{0,8},{1,9},{2,10},{3,11},{4,12},{5,13},{6,14},{7,15},{8,16},{9,17... | collective-permute-start | bytes 1572872 | tf_op jit(solution)/shard_map/ppermute | solution.py:59
  134.7 14.9 %collective-permute-start.5 = (bf16[4,128,512]{2,1,0:T(8,128)(2,1)}, bf16[4,128,512]{2,1,0:T(8,128)(2,1)}, u32[]{:S(2)}, u32[]{:S(2)}) collective-permute-start(bf16[4,128,512]{2,1,0:T(8,128)(2,1)} %fusion.1327), channel_id=1, source_target_pairs={{0,8},{1,9},{2,10},{3,11},{4,12},{5,13},{6,14},{7,15},{8,16},{9,17... | collective-permute-start | bytes 1572872 | tf_op jit(solution)/shard_map/ppermute | solution.py:58
  149.6 31.4 %collective-permute-start.10 = (bf16[4,512,128]{2,1,0:T(8,128)(2,1)}, bf16[4,512,128]{2,1,0:T(8,128)(2,1)}, u32[]{:S(2)}, u32[]{:S(2)}) collective-permute-start(bf16[4,512,128]{2,1,0:T(8,128)(2,1)} %get-tuple-element.38), channel_id=1, source_target_pairs={{0,16},{1,17},{2,18},{3,19},{4,20},{5,21},{6,22},{7,23},{8,24},{9,... | collective-permute-start | bytes 1572872 | tf_op jit(solution)/shard_map/ppermute | solution.py:59
  171.2 20.4 %copy-start.16 = (f32[1,128,512]{2,1,0:T(8,128)}, f32[1,128,512]{2,1,0:T(8,128)S(1)}, u32[]{:S(2)}) copy-start(f32[1,128,512]{2,1,0:T(8,128)S(1)} %convolution_bitcast_fusion.93) | copy-start | bytes 786436
  171.2 20.4 %collective-permute-start.7 = (bf16[4,128,512]{2,1,0:T(8,128)(2,1)}, bf16[4,128,512]{2,1,0:T(8,128)(2,1)}, u32[]{:S(2)}, u32[]{:S(2)}) collective-permute-start(bf16[4,128,512]{2,1,0:T(8,128)(2,1)} %get-tuple-element.40), channel_id=1, source_target_pairs={{0,16},{1,17},{2,18},{3,19},{4,20},{5,21},{6,22},{7,23},{8,24},{9,... | collective-permute-start | bytes 1572872 | tf_op jit(solution)/shard_map/ppermute | solution.py:58
  183.9 40.0 %collective-permute-start.12 = (bf16[4,512,128]{2,1,0:T(8,128)(2,1)}, bf16[4,512,128]{2,1,0:T(8,128)(2,1)}, u32[]{:S(2)}, u32[]{:S(2)}) collective-permute-start(bf16[4,512,128]{2,1,0:T(8,128)(2,1)} %fusion.1324), channel_id=1, source_target_pairs={{0,32},{1,33},{2,34},{3,35},{4,36},{5,37},{6,38},{7,39},{8,40},{9,... | collective-permute-start | bytes 1572872 | tf_op jit(solution)/shard_map/ppermute | solution.py:59
  213.6 20.5 %collective-permute-start.9 = (bf16[4,128,512]{2,1,0:T(8,128)(2,1)}, bf16[4,128,512]{2,1,0:T(8,128)(2,1)}, u32[]{:S(2)}, u32[]{:S(2)}) collective-permute-start(bf16[4,128,512]{2,1,0:T(8,128)(2,1)} %fusion.1325), channel_id=1, source_target_pairs={{0,32},{1,33},{2,34},{3,35},{4,36},{5,37},{6,38},{7,39},{8,40},{9,... | collective-permute-start | bytes 1572872 | tf_op jit(solution)/shard_map/ppermute | solution.py:58
  228.3 34.5 %collective-permute-start.14 = (bf16[4,512,128]{2,1,0:T(8,128)(2,1)}, bf16[4,512,128]{2,1,0:T(8,128)(2,1)}, u32[]{:S(2)}, u32[]{:S(2)}) collective-permute-start(bf16[4,512,128]{2,1,0:T(8,128)(2,1)} %get-tuple-element.34), channel_id=1, source_target_pairs={{0,64},{1,65},{2,66},{3,67},{4,68},{5,69},{6,70},{7,71},{8,72},{9,... | collective-permute-start | bytes 1572872 | tf_op jit(solution)/shard_map/ppermute | solution.py:59
  255.7 42.9 %copy-start.18 = (f32[1,128,512]{2,1,0:T(8,128)}, f32[1,128,512]{2,1,0:T(8,128)S(1)}, u32[]{:S(2)}) copy-start(f32[1,128,512]{2,1,0:T(8,128)S(1)} %convolution_bitcast_fusion.77) | copy-start | bytes 786436
  255.7 42.9 %collective-permute-start.11 = (bf16[4,128,512]{2,1,0:T(8,128)(2,1)}, bf16[4,128,512]{2,1,0:T(8,128)(2,1)}, u32[]{:S(2)}, u32[]{:S(2)}) collective-permute-start(bf16[4,128,512]{2,1,0:T(8,128)(2,1)} %get-tuple-element.36), channel_id=1, source_target_pairs={{0,64},{1,65},{2,66},{3,67},{4,68},{5,69},{6,70},{7,71},{8,72},{9,... | collective-permute-start | bytes 1572872 | tf_op jit(solution)/shard_map/ppermute | solution.py:58
  260.7 37.9 %copy-start.30 = (f32[1,128,512]{2,1,0:T(8,128)}, f32[1,128,512]{2,1,0:T(8,128)S(1)}, u32[]{:S(2)}) copy-start(f32[1,128,512]{2,1,0:T(8,128)S(1)} %convolution_bitcast_fusion.76) | copy-start | bytes 786436
  262.8 35.8 %copy-start.64 = (f32[1,128,512]{2,1,0:T(8,128)S(1)}, f32[1,128,512]{2,1,0:T(8,128)}, u32[]{:S(2)}) copy-start(f32[1,128,512]{2,1,0:T(8,128)} %convolution_bitcast_fusion.79) | copy-start | bytes 786436
  265.8 54.5 %collective-permute-start.16 = (bf16[4,512,128]{2,1,0:T(8,128)(2,1)}, bf16[4,512,128]{2,1,0:T(8,128)(2,1)}, u32[]{:S(2)}, u32[]{:S(2)}) collective-permute-start(bf16[4,512,128]{2,1,0:T(8,128)(2,1)} %fusion.1322), channel_id=1, source_target_pairs={{0,128},{1,129},{2,130},{3,131},{4,132},{5,133},{6,134},{7,135},{8... | collective-permute-start | bytes 1572872 | tf_op jit(solution)/shard_map/ppermute | solution.py:59
  314.3 14.9 %collective-permute-start.13 = (bf16[4,128,512]{2,1,0:T(8,128)(2,1)S(1)}, bf16[4,128,512]{2,1,0:T(8,128)(2,1)}, u32[]{:S(2)}, u32[]{:S(2)}) collective-permute-start(bf16[4,128,512]{2,1,0:T(8,128)(2,1)S(1)} %fusion.1323), channel_id=1, source_target_pairs={{0,128},{1,129},{2,130},{3,131},{4,132},{5,133},{6,134},{7,135},{8... | collective-permute-start | bytes 1572872 | tf_op jit(solution)/shard_map/ppermute | solution.py:58
  324.9 25.3 %collective-permute-start.18 = (bf16[4,512,128]{2,1,0:T(8,128)(2,1)}, bf16[4,512,128]{2,1,0:T(8,128)(2,1)}, u32[]{:S(2)}, u32[]{:S(2)}) collective-permute-start(bf16[4,512,128]{2,1,0:T(8,128)(2,1)} %get-tuple-element.30), channel_id=1, source_target_pairs={{0,1},{1,2},{2,3},{3,4},{4,5},{5,6},{6,7},{7,8},{8,9},{9,10},{10,1... | collective-permute-start | bytes 1572872 | tf_op jit(solution)/shard_map/ppermute | solution.py:59
  344.9 8.7 %collective-permute-start.15 = (bf16[4,128,512]{2,1,0:T(8,128)(2,1)S(1)}, bf16[4,128,512]{2,1,0:T(8,128)(2,1)}, u32[]{:S(2)}, u32[]{:S(2)}) collective-permute-start(bf16[4,128,512]{2,1,0:T(8,128)(2,1)S(1)} %get-tuple-element.32), channel_id=1, source_target_pairs={{0,1},{1,2},{2,3},{3,4},{4,5},{5,6},{6,7},{7,8},{8,9},{9,10},{10,1... | collective-permute-start | bytes 1572872 | tf_op jit(solution)/shard_map/ppermute | solution.py:58
  353.3 28.4 %collective-permute-start.20 = (bf16[4,512,128]{2,1,0:T(8,128)(2,1)}, bf16[4,512,128]{2,1,0:T(8,128)(2,1)}, u32[]{:S(2)}, u32[]{:S(2)}) collective-permute-start(bf16[4,512,128]{2,1,0:T(8,128)(2,1)} %fusion.1320), channel_id=1, source_target_pairs={{0,2},{1,3},{2,4},{3,5},{4,6},{5,7},{6,8},{7,9},{8,10},{9,11},{10,... | collective-permute-start | bytes 1572872 | tf_op jit(solution)/shard_map/ppermute | solution.py:59
  375.6 14.9 %collective-permute-start.17 = (bf16[4,128,512]{2,1,0:T(8,128)(2,1)}, bf16[4,128,512]{2,1,0:T(8,128)(2,1)}, u32[]{:S(2)}, u32[]{:S(2)}) collective-permute-start(bf16[4,128,512]{2,1,0:T(8,128)(2,1)} %fusion.1321), channel_id=1, source_target_pairs={{0,2},{1,3},{2,4},{3,5},{4,6},{5,7},{6,8},{7,9},{8,10},{9,11},{10,... | collective-permute-start | bytes 1572872 | tf_op jit(solution)/shard_map/ppermute | solution.py:58
  386.2 30.7 %collective-permute-start.22 = (bf16[4,512,128]{2,1,0:T(8,128)(2,1)}, bf16[4,512,128]{2,1,0:T(8,128)(2,1)}, u32[]{:S(2)}, u32[]{:S(2)}) collective-permute-start(bf16[4,512,128]{2,1,0:T(8,128)(2,1)} %get-tuple-element.26), channel_id=1, source_target_pairs={{0,4},{1,5},{2,6},{3,7},{4,8},{5,9},{6,10},{7,11},{8,12},{9,13},{1... | collective-permute-start | bytes 1572872 | tf_op jit(solution)/shard_map/ppermute | solution.py:59
  412.2 20.9 %copy-start.22 = (f32[1,128,512]{2,1,0:T(8,128)}, f32[1,128,512]{2,1,0:T(8,128)S(1)}, u32[]{:S(2)}) copy-start(f32[1,128,512]{2,1,0:T(8,128)S(1)} %convolution_bitcast_fusion.45) | copy-start | bytes 786436
  412.2 20.8 %collective-permute-start.19 = (bf16[4,128,512]{2,1,0:T(8,128)(2,1)}, bf16[4,128,512]{2,1,0:T(8,128)(2,1)}, u32[]{:S(2)}, u32[]{:S(2)}) collective-permute-start(bf16[4,128,512]{2,1,0:T(8,128)(2,1)} %get-tuple-element.28), channel_id=1, source_target_pairs={{0,4},{1,5},{2,6},{3,7},{4,8},{5,9},{6,10},{7,11},{8,12},{9,13},{1... | collective-permute-start | bytes 1572872 | tf_op jit(solution)/shard_map/ppermute | solution.py:58
  414.8 18.3 %copy-start.34 = (f32[1,128,512]{2,1,0:T(8,128)}, f32[1,128,512]{2,1,0:T(8,128)S(1)}, u32[]{:S(2)}) copy-start(f32[1,128,512]{2,1,0:T(8,128)S(1)} %convolution_bitcast_fusion.44) | copy-start | bytes 786436
  419.9 41.2 %collective-permute-start.24 = (bf16[4,512,128]{2,1,0:T(8,128)(2,1)}, bf16[4,512,128]{2,1,0:T(8,128)(2,1)}, u32[]{:S(2)}, u32[]{:S(2)}) collective-permute-start(bf16[4,512,128]{2,1,0:T(8,128)(2,1)} %fusion.1318), channel_id=1, source_target_pairs={{0,8},{1,9},{2,10},{3,11},{4,12},{5,13},{6,14},{7,15},{8,16},{9,17... | collective-permute-start | bytes 1572872 | tf_op jit(solution)/shard_map/ppermute | solution.py:59
  455.1 23.0 %collective-permute-start.21 = (bf16[4,128,512]{2,1,0:T(8,128)(2,1)}, bf16[4,128,512]{2,1,0:T(8,128)(2,1)}, u32[]{:S(2)}, u32[]{:S(2)}) collective-permute-start(bf16[4,128,512]{2,1,0:T(8,128)(2,1)} %fusion.1319), channel_id=1, source_target_pairs={{0,8},{1,9},{2,10},{3,11},{4,12},{5,13},{6,14},{7,15},{8,16},{9,17... | collective-permute-start | bytes 1572872 | tf_op jit(solution)/shard_map/ppermute | solution.py:58
  461.0 17.1 %copy-start.82 = (f32[1,128,512]{2,1,0:T(8,128)S(1)}, f32[1,128,512]{2,1,0:T(8,128)}, u32[]{:S(2)}) copy-start(f32[1,128,512]{2,1,0:T(8,128)} %convolution_bitcast_fusion.37) | copy-start | bytes 786436
  461.0 17.1 %copy-start.90 = (f32[1,128,512]{2,1,0:T(8,128)S(1)}, f32[1,128,512]{2,1,0:T(8,128)}, u32[]{:S(2)}) copy-start(f32[1,128,512]{2,1,0:T(8,128)} %convolution_bitcast_fusion.36) | copy-start | bytes 786436
  465.6 44.0 %copy-start.3 = (f32[4,512,128]{2,1,0:T(8,128)}, f32[4,512,128]{2,1,0:T(8,128)S(1)}, u32[]{:S(2)}) copy-start(f32[4,512,128]{2,1,0:T(8,128)S(1)} %get-tuple-element.23) | copy-start | bytes 3145732
  465.6 44.0 %collective-permute-start.26 = (bf16[4,512,128]{2,1,0:T(8,128)(2,1)}, bf16[4,512,128]{2,1,0:T(8,128)(2,1)}, u32[]{:S(2)}, u32[]{:S(2)}) collective-permute-start(bf16[4,512,128]{2,1,0:T(8,128)(2,1)} %get-tuple-element.22), channel_id=1, source_target_pairs={{0,16},{1,17},{2,18},{3,19},{4,20},{5,21},{6,22},{7,23},{8,24},{9,... | collective-permute-start | bytes 1572872 | tf_op jit(solution)/shard_map/ppermute | solution.py:59
  499.9 18.6 %copy-start.24 = (f32[1,128,512]{2,1,0:T(8,128)}, f32[1,128,512]{2,1,0:T(8,128)S(1)}, u32[]{:S(2)}) copy-start(f32[1,128,512]{2,1,0:T(8,128)S(1)} %convolution_bitcast_fusion.29) | copy-start | bytes 786436
  499.9 18.6 %collective-permute-start.23 = (bf16[4,128,512]{2,1,0:T(8,128)(2,1)}, bf16[4,128,512]{2,1,0:T(8,128)(2,1)}, u32[]{:S(2)}, u32[]{:S(2)}) collective-permute-start(bf16[4,128,512]{2,1,0:T(8,128)(2,1)} %get-tuple-element.24), channel_id=1, source_target_pairs={{0,16},{1,17},{2,18},{3,19},{4,20},{5,21},{6,22},{7,23},{8,24},{9,... | collective-permute-start | bytes 1572872 | tf_op jit(solution)/shard_map/ppermute | solution.py:58
  512.6 41.7 %collective-permute-start.28 = (bf16[4,512,128]{2,1,0:T(8,128)(2,1)}, bf16[4,512,128]{2,1,0:T(8,128)(2,1)}, u32[]{:S(2)}, u32[]{:S(2)}) collective-permute-start(bf16[4,512,128]{2,1,0:T(8,128)(2,1)} %fusion.1316), channel_id=1, source_target_pairs={{0,32},{1,33},{2,34},{3,35},{4,36},{5,37},{6,38},{7,39},{8,40},{9,... | collective-permute-start | bytes 1572872 | tf_op jit(solution)/shard_map/ppermute | solution.py:59
  540.5 21.7 %collective-permute-start.25 = (bf16[4,128,512]{2,1,0:T(8,128)(2,1)}, bf16[4,128,512]{2,1,0:T(8,128)(2,1)}, u32[]{:S(2)}, u32[]{:S(2)}) collective-permute-start(bf16[4,128,512]{2,1,0:T(8,128)(2,1)} %fusion.1317), channel_id=1, source_target_pairs={{0,32},{1,33},{2,34},{3,35},{4,36},{5,37},{6,38},{7,39},{8,40},{9,... | collective-permute-start | bytes 1572872 | tf_op jit(solution)/shard_map/ppermute | solution.py:58
  558.8 29.9 %collective-permute-start.30 = (bf16[4,512,128]{2,1,0:T(8,128)(2,1)}, bf16[4,512,128]{2,1,0:T(8,128)(2,1)}, u32[]{:S(2)}, u32[]{:S(2)}) collective-permute-start(bf16[4,512,128]{2,1,0:T(8,128)(2,1)} %get-tuple-element.18), channel_id=1, source_target_pairs={{0,64},{1,65},{2,66},{3,67},{4,68},{5,69},{6,70},{7,71},{8,72},{9,... | collective-permute-start | bytes 1572872 | tf_op jit(solution)/shard_map/ppermute | solution.py:59
  583.8 27.4 %collective-permute-start.27 = (bf16[4,128,512]{2,1,0:T(8,128)(2,1)}, bf16[4,128,512]{2,1,0:T(8,128)(2,1)}, u32[]{:S(2)}, u32[]{:S(2)}) collective-permute-start(bf16[4,128,512]{2,1,0:T(8,128)(2,1)} %get-tuple-element.20), channel_id=1, source_target_pairs={{0,64},{1,65},{2,66},{3,67},{4,68},{5,69},{6,70},{7,71},{8,72},{9,... | collective-permute-start | bytes 1572872 | tf_op jit(solution)/shard_map/ppermute | solution.py:58
  588.7 22.5 %copy-start.52 = (f32[1,128,512]{2,1,0:T(8,128)S(1)}, f32[1,128,512]{2,1,0:T(8,128)}, u32[]{:S(2)}) copy-start(f32[1,128,512]{2,1,0:T(8,128)} %convolution_bitcast_fusion.15) | copy-start | bytes 786436
  591.6 87.5 %collective-permute-start.31 = (bf16[4,512,128]{2,1,0:T(8,128)(2,1)}, bf16[4,512,128]{2,1,0:T(8,128)(2,1)}, u32[]{:S(2)}, u32[]{:S(2)}) collective-permute-start(bf16[4,512,128]{2,1,0:T(8,128)(2,1)} %fusion.1314), channel_id=1, source_target_pairs={{0,128},{1,129},{2,130},{3,131},{4,132},{5,133},{6,134},{7,135},{8... | collective-permute-start | bytes 1572872 | tf_op jit(solution)/shard_map/ppermute | solution.py:59
  626.7 56.9 %collective-permute-start.29 = (bf16[4,128,512]{2,1,0:T(8,128)(2,1)S(1)}, bf16[4,128,512]{2,1,0:T(8,128)(2,1)}, u32[]{:S(2)}, u32[]{:S(2)}) collective-permute-start(bf16[4,128,512]{2,1,0:T(8,128)(2,1)S(1)} %fusion.1315), channel_id=1, source_target_pairs={{0,128},{1,129},{2,130},{3,131},{4,132},{5,133},{6,134},{7,135},{8... | collective-permute-start | bytes 1572872 | tf_op jit(solution)/shard_map/ppermute | solution.py:58
  (115 other events, 695.5 us)
where the time goes:
time: 702 us; the launch traced here: 688 us
  matrix products  333 us (47%)
  waiting for transfers between devices  143 us (20%)
  other arithmetic  125 us (18%)
  starting transfers between devices  58.4 us (8%)
  between operations  14.7 us (2%)
  local copies, waits for them, and re-layouts  14.3 us (2%)
    ppermute x16, waiting for transfers between devices, device_run(): peer_one = lax.ppermute(one_bf, ('outer', 'inner'), send_pairs)  143 us
    dot_general x64, matrix products, replica_grads(): jnp.dot(act_bf, two_bf[layer_idx], preferred_element_type=jnp.float32)  71.4 us
    dot_general x64, matrix products, replica_grads(): lax.dot_general(normed, d_pre, row_dims, preferred_element_type=jnp.float32)  62.1 us
    convert_element_type x17, other arithmetic, device_run(): two_bf = w_two.astype(jnp.bfloat16)  57.2 us
    dot_general x64, matrix products, replica_grads(): jnp.dot(normed, one_bf[layer_idx], preferred_element_type=jnp.float32)  55.6 us
    dot_general x48, matrix products, replica_grads(): lax.dot_general(d_out, two_bf[layer_idx], feat_dims, preferred_element_ty...  50.6 us
    dot_general x64, matrix products, replica_grads(): lax.dot_general(act_bf, d_out, row_dims, preferred_element_type=jnp.float32)  50.3 us
    convert_element_type x17, other arithmetic, device_run(): one_bf = w_one.astype(jnp.bfloat16)  45.8 us
  transfers between devices with their start and end apart: 32, of which 10 were waited for; matrix products, arithmetic and copies ran while one was open for 66% of the time, Pallas kernels for 0%

commit v1 on v0

v1 whole, which is shorter than its diff:
```python
import jax
import jax.numpy as jnp
from jax import lax
from jax.experimental import pallas as pl
from jax.experimental.pallas import tpu as pltpu
from jax.sharding import PartitionSpec as P

RMS_EPS = 1e-6
RATE_BASE = 1.5
MESH = pl.DeviceIdType.MESH
GELU_A = 0.7978845608028654
GELU_B = 0.7978845608028654 * 0.044715


def two_power(k):
    return (1 + k % 2) * (1 + 3 * ((k // 2) % 2)) * (1 + 15 * (k // 4))


def run_kernel(n_dev, n_inner, mix_ref, a_hbm, t_hbm, w1_hbm, w2_hbm, o1_hbm, o2_hbm,
               a_ref, t_ref, w1, w2, q1, q2, r1, r2, xs, us, gs, hs, invs,
               io_sem, send_sem, recv_sem):
    n_steps, rows, feat = a_ref.shape
    n_layers = w1.shape[0]
    log_g = n_dev.bit_length() - 1
    rate = RATE_BASE / n_layers
    me = lax.axis_index('outer') * n_inner + lax.axis_index('inner')
    n_chunks = 2 * n_layers

    def as_id(r):
        return (r // n_inner, r % n_inner)

    def load_in(c):
        l, m = c // 2, c % 2
        src, dst = (w1_hbm, w1) if m == 0 else (w2_hbm, w2)
        return pltpu.make_async_copy(src.at[l], dst.at[l], io_sem.at[c])

    def load_out(c):
        l, m = c // 2, c % 2
        src, dst = (w1, o1_hbm) if m == 0 else (w2, o2_hbm)
        return pltpu.make_async_copy(src.at[l], dst.at[l], io_sem.at[c])

    in_a = pltpu.make_async_copy(a_hbm, a_ref, io_sem.at[n_chunks])
    in_t = pltpu.make_async_copy(t_hbm, t_ref, io_sem.at[n_chunks + 1])
    for c in range(n_chunks):
        load_in(c).start()
    in_a.start()
    in_t.start()

    barrier = pltpu.get_barrier_semaphore()
    for k in range(log_g):
        pl.semaphore_signal(barrier, inc=1, device_id=as_id((me + n_dev - 2 ** k) % n_dev), device_id_type=MESH)

    def send(t, c):
        l, m = c // 2, c % 2
        peer = (me + two_power(t % log_g)) % n_dev
        src, dst = (q1, r1) if m == 0 else (q2, r2)
        return pltpu.make_async_remote_copy(
            src.at[t % 2, l], dst.at[t, l], send_sem.at[t % 2, c], recv_sem.at[t, c],
            device_id=as_id(peer), device_id_type=MESH)

    for c in range(n_chunks):
        l, m = c // 2, c % 2
        load_in(c).wait()
        if m == 0:
            q1[0, l] = w1[l].astype(jnp.bfloat16)
        else:
            q2[0, l] = w2[l].astype(jnp.bfloat16)
        if c == 0:
            pl.semaphore_wait(barrier, log_g)
        else:
            send(0, c - 1).start()
    in_a.wait()
    in_t.wait()

    row_dims = (((0,), (0,)), ((), ()))
    feat_dims = (((1,), (1,)), ((), ()))

    def step(t, carry):
        slot = t % 2
        nxt = 1 - slot
        self_w = mix_ref[t]
        peer_w = 1.0 - self_w
        hid = a_ref[t].astype(jnp.float32)
        for l in range(n_layers):
            inv = lax.rsqrt(jnp.mean(hid * hid, axis=-1, keepdims=True) + RMS_EPS)
            normed = (hid * inv).astype(jnp.bfloat16)
            z = jnp.dot(normed, q1[slot, l], preferred_element_type=jnp.float32)
            z2 = z * z
            th = jnp.tanh(z * (GELU_A + GELU_B * z2))
            half = 0.5 * z
            act = (half + half * th).astype(jnp.bfloat16)
            gs[l] = 0.5 + 0.5 * th + half * (1.0 - th * th) * (GELU_A + (3.0 * GELU_B) * z2)
            us[l] = act
            xs[l] = normed
            hs[l] = hid
            invs[l] = jnp.broadcast_to(inv, (rows, feat))
            out = jnp.dot(act, q2[slot, l], preferred_element_type=jnp.float32)
            hid = (hid + out).astype(jnp.bfloat16).astype(jnp.float32)
            if l == 0:
                send(t, n_chunks - 1).start()
        d_hid = (2.0 / (rows * feat)) * (hid - t_ref[t].astype(jnp.float32))
        for l in reversed(range(n_layers)):
            d_out = d_hid.astype(jnp.bfloat16)
            d_act = lax.dot_general(d_out, q2[slot, l], feat_dims, preferred_element_type=jnp.float32)
            d_pre = (d_act * gs[l]).astype(jnp.bfloat16)
            g2 = lax.dot_general(us[l], d_out, row_dims, preferred_element_type=jnp.float32)
            w2[l] = self_w * w2[l] - rate * g2
            if l > 0:
                d_norm = lax.dot_general(d_pre, q1[slot, l], feat_dims, preferred_element_type=jnp.float32)
                inv = invs[l]
                hid_l = hs[l]
                d_hid = d_hid + inv * d_norm - (inv * inv * inv) * hid_l * jnp.mean(d_norm * hid_l, axis=-1, keepdims=True)
            g1 = lax.dot_general(xs[l], d_pre, row_dims, preferred_element_type=jnp.float32)
            w1[l] = self_w * w1[l] - rate * g1

        more = t < n_steps - 1
        for c in range(n_chunks):
            l, m = c // 2, c % 2
            send(t, c).wait_recv()

            @pl.when(t > 0)
            def _():
                send(t - 1, c).wait_send()

            if m == 0:
                new = w1[l] + peer_w * r1[t, l].astype(jnp.float32)
                w1[l] = new
                q1[nxt, l] = new.astype(jnp.bfloat16)
            else:
                new = w2[l] + peer_w * r2[t, l].astype(jnp.float32)
                w2[l] = new
                q2[nxt, l] = new.astype(jnp.bfloat16)
            if c > 0:
                @pl.when(more)
                def _():
                    send(t + 1, c - 1).start()
        return carry

    lax.fori_loop(0, n_steps, step, 0)
    for c in range(n_chunks):
        load_out(c).start()
    for c in range(n_chunks):
        send(n_steps - 1, c).wait_send()
        load_out(c).wait()


def solution(mesh):
    n_inner = mesh.shape['inner']
    n_dev = mesh.shape['outer'] * n_inner
    spec = P('outer', 'inner')

    def device_run(w_one, w_two, inputs, targets, mix_self):
        n_layers, feat, wide = w_one.shape[2:]
        n_steps, rows = inputs.shape[2:4]
        bf, f32 = jnp.bfloat16, jnp.float32
        out_one, out_two = pl.pallas_call(
            lambda *refs: run_kernel(n_dev, n_inner, *refs),
            out_shape=(jax.ShapeDtypeStruct((n_layers, feat, wide), f32), jax.ShapeDtypeStruct((n_layers, wide, feat), f32)),
            in_specs=[pl.BlockSpec(memory_space=pltpu.SMEM)] + [pl.BlockSpec(memory_space=pl.ANY)] * 4,
            out_specs=(pl.BlockSpec(memory_space=pl.ANY),) * 2,
            scratch_shapes=[
                pltpu.VMEM((n_steps, rows, feat), bf), pltpu.VMEM((n_steps, rows, feat), bf),
                pltpu.VMEM((n_layers, feat, wide), f32), pltpu.VMEM((n_layers, wide, feat), f32),
                pltpu.VMEM((2, n_layers, feat, wide), bf), pltpu.VMEM((2, n_layers, wide, feat), bf),
                pltpu.VMEM((n_steps, n_layers, feat, wide), bf), pltpu.VMEM((n_steps, n_layers, wide, feat), bf),
                pltpu.VMEM((n_layers, rows, feat), bf), pltpu.VMEM((n_layers, rows, wide), bf),
                pltpu.VMEM((n_layers, rows, wide), f32), pltpu.VMEM((n_layers, rows, feat), f32),
                pltpu.VMEM((n_layers, rows, feat), f32),
                pltpu.SemaphoreType.DMA((2 * n_layers + 2,)), pltpu.SemaphoreType.DMA((2, 2 * n_layers)),
                pltpu.SemaphoreType.DMA((n_steps, 2 * n_layers)),
            ],
            compiler_params=pltpu.CompilerParams(collective_id=0, has_side_effects=True, vmem_limit_bytes=48 * 1024 * 1024),
            name="gossip_run",
        )(mix_self[0, 0], inputs[0, 0], targets[0, 0], w_one[0, 0], w_two[0, 0])
        return out_one[None, None], out_two[None, None]

    return jax.shard_map(device_run, mesh=mesh, in_specs=(spec,) * 5, out_specs=(spec, spec), check_vma=False)
```

time: 702 us -> 514 us (0.73)
  the two profiles are of different devices: /device:TPU:54 before, /device:TPU:63 now
where the time goes in v1:
time: 514 us
  Pallas kernels  506 us (98%)
  local copies, waits for them, and re-layouts  6.94 us (1%)
    pallas_call x1, Pallas kernels, device_run(): pl.pallas_call(lambda *refs: run_kernel(n_dev, n_inner, *refs), out_shape...  506 us

profile of v1, /device:TPU:63, one launch (start us, length us, event | category | flops | bytes accessed | tf_op | source)
XLA Modules:
  0.0 514.0 jit_solution(9588911310632130268)
XLA Ops:
  0.6 0.0 copy-start.4
  0.6 0.6 copy-done.4
  1.3 0.0 copy-start
  1.3 1.2 copy-done
  2.5 0.0 copy-start.1
  2.5 1.2 copy-done.1
  3.7 0.0 copy-start.2
  3.7 0.9 copy-done.2
  4.7 0.0 copy-start.3
  4.7 0.9 copy-done.3
  5.6 506.4 %gossip_run.1 = (f32[4,128,512]{2,1,0:T(8,128)S(1)}, f32[4,512,128]{2,1,0:T(8,128)S(1)}) custom-call(f32[16]{0:T(128)S(1)} %bitcast.13, bf16[16,64,128]{2,1,0:T(8,128)(2,1)S(1)} %bitcast.11, bf16[16,64,128]{2,1,0:T(8,128)(2,1)S(1)} %bitcast.12, f32[4,128,512]{2,1,0:T(8,128)S(1)} %bitcast.7, f32[4,512,128]{2,1,0:T(8,128)S(1)} %bitcast.8), custom_call_target="tpu_custom_call" | custom-call | tf_op jit(solution)/shard_map/gossip_run/pallas_call | solution.py:156
  512.1 1.0 copy.9
  513.1 1.0 copy.10
Async XLA Ops:
  0.6 0.7 copy-start.4
  1.3 1.2 copy-start
  2.5 1.2 copy-start.1
  3.7 0.9 copy-start.2
  4.7 0.9 copy-start.3

commit v2 on v1

--- a/solution.py
+++ b/solution.py
@@ -11,22 +11,32 @@
 GELU_A = 0.7978845608028654
 GELU_B = 0.7978845608028654 * 0.044715
 
+ROUTES = (
+    {2: (2,) * 8, 4: (0, 1) * 4, 6: (0, 0, 0, 3) * 2, 7: (3,) * 8},
+    {1: (1,) * 8, 2: (0, 1) * 4, 3: (0, 1, 0, 0) * 2, 4: (1, 0) * 4},
+)
+GATES = ((1, 1, 2), (1, 3, 4), (1, 5, 6), (1, 9, 10), (1, 11, 12), (1, 13, 14))
+RELAY_AHEAD = 5
+
 
 def two_power(k):
     return (1 + k % 2) * (1 + 3 * ((k // 2) % 2)) * (1 + 15 * (k // 4))
 
 
 def run_kernel(n_dev, n_inner, mix_ref, a_hbm, t_hbm, w1_hbm, w2_hbm, o1_hbm, o2_hbm,
-               a_ref, t_ref, w1, w2, q1, q2, r1, r2, xs, us, gs, hs, invs,
-               io_sem, send_sem, recv_sem):
+               a_ref, t_ref, w1, w2, q1, q2, r1, r2, p1, p2, xs, us, gs, hs, invs,
+               io_sem, send_sem, recv_sem, pass_sem, pass_recv_sem, gate_sem):
     n_steps, rows, feat = a_ref.shape
     n_layers = w1.shape[0]
     log_g = n_dev.bit_length() - 1
     rate = RATE_BASE / n_layers
     me = lax.axis_index('outer') * n_inner + lax.axis_index('inner')
+    core = me % 2
+    plane_pos, line_pos = me % 32, me % 8
     n_chunks = 2 * n_layers
 
     def as_id(r):
+        r = r % n_dev
         return (r // n_inner, r % n_inner)
 
     def load_in(c):
@@ -46,17 +56,80 @@
     in_a.start()
     in_t.start()
 
+    offsets = sorted({2 ** k for k in range(log_g)} | {2 ** k - 32 + n_dev for k in range(1, 5)}
+                     | {2 ** k - 8 + n_dev for k in range(1, 3)} | {n_dev - 96, n_dev - 64})
     barrier = pltpu.get_barrier_semaphore()
-    for k in range(log_g):
-        pl.semaphore_signal(barrier, inc=1, device_id=as_id((me + n_dev - 2 ** k) % n_dev), device_id_type=MESH)
-
-    def send(t, c):
-        l, m = c // 2, c % 2
-        peer = (me + two_power(t % log_g)) % n_dev
-        src, dst = (q1, r1) if m == 0 else (q2, r2)
-        return pltpu.make_async_remote_copy(
-            src.at[t % 2, l], dst.at[t, l], send_sem.at[t % 2, c], recv_sem.at[t, c],
-            device_id=as_id(peer), device_id_type=MESH)
+    for off in offsets:
+        pl.semaphore_signal(barrier, inc=1, device_id=as_id(me + n_dev - off), device_id_type=MESH)
+
+    def kinds(k):
+        out = [0] * n_chunks
+        for cls in range(2):
+            for step_k, row in ROUTES[cls].items():
+                here = jnp.where((k == step_k) & (core == cls), 1, 0)
+                out = [o + v * here if v else o for o, v in zip(out, row)]
+        return out
+
+    def own_buf(c):
+        return (q1, r1, p1) if c % 2 == 0 else (q2, r2, p2)
+
+    def start_send(t, k, shift, kind, c):
+        l = c // 2
+        own, final, relay = own_buf(c)
+
+        def go(dst, sem, to):
+            pltpu.make_async_remote_copy(own.at[t % 2, l], dst.at[t, l], send_sem.at[t % 2, c], sem.at[t, c],
+                                         device_id=as_id(to), device_id_type=MESH).start()
+
+        if isinstance(kind, int):
+            go(final, recv_sem, me + shift)
+            return
+        via_plane = (kind == 1) & (plane_pos + shift >= 32)
+        via_line = (kind == 2) & (line_pos + shift >= 8)
+        via_back = kind == 3
+        via = via_plane | via_line | via_back
+        stop = jnp.where(via_plane, me + shift - 32, jnp.where(via_line, me + shift - 8, me - jnp.where(k == 6, 96, 64)))
+
+        @pl.when(via)
+        def _():
+            go(relay, pass_recv_sem, stop + n_dev)
+
+        @pl.when(jnp.logical_not(via))
+        def _():
+            go(final, recv_sem, me + shift)
+
+    def wait_sent(t, c):
+        own, final, _ = own_buf(c)
+        pltpu.make_async_remote_copy(own.at[t % 2, c // 2], final.at[t, c // 2], send_sem.at[t % 2, c], recv_sem.at[t, c],
+                                     device_id=as_id(me + 1), device_id_type=MESH).wait_send()
+
+    def wait_arrived(t, c):
+        own, final, _ = own_buf(c)
+        pltpu.make_async_remote_copy(own.at[t % 2, c // 2], final.at[t, c // 2], send_sem.at[t % 2, c], recv_sem.at[t, c],
+                                     device_id=as_id(me + 1), device_id_type=MESH).wait_recv()
+
+    def pass_copy(t, c, to):
+        _, final, relay = own_buf(c)
+        return pltpu.make_async_remote_copy(relay.at[t, c // 2], final.at[t, c // 2], pass_sem.at[t % 2, c], recv_sem.at[t, c],
+                                            device_id=as_id(to), device_id_type=MESH)
+
+    def pass_in(t, c):
+        _, final, relay = own_buf(c)
+        return pltpu.make_async_remote_copy(relay.at[t, c // 2], relay.at[t, c // 2], pass_sem.at[t % 2, c], pass_recv_sem.at[t, c],
+                                            device_id=as_id(me + 1), device_id_type=MESH)
+
+    def pass_roles(k, shift, kind_row):
+        out = []
+        for kind in kind_row:
+            if isinstance(kind, int):
+                out.append(None)
+                continue
+            plane = (kind == 1) & (plane_pos < shift)
+            line = (kind == 2) & (line_pos < shift)
+            back = kind == 3
+            to = me + jnp.where(plane, 32, jnp.where(line, 8, n_dev - jnp.where(k == 6, 96, 64)))
+            out.append((jnp.where(plane | line | back, 1, 0), to))
+        return out
 
     for c in range(n_chunks):
         l, m = c // 2, c % 2
@@ -66,18 +139,22 @@
         else:
             q2[0, l] = w2[l].astype(jnp.bfloat16)
         if c == 0:
-            pl.semaphore_wait(barrier, log_g)
+            pl.semaphore_wait(barrier, len(offsets))
         else:
-            send(0, c - 1).start()
+            start_send(0, 0, 1, 0, c - 1)
     in_a.wait()
     in_t.wait()
 
     row_dims = (((0,), (0,)), ((), ()))
     feat_dims = (((1,), (1,)), ((), ()))
 
-    def step(t, carry):
+    def step(t, passed):
         slot = t % 2
         nxt = 1 - slot
+        k = t % log_g
+        k_next = (t + 1) % log_g
+        shift, shift_next = two_power(k), two_power(k_next)
+        kind_now, kind_next = kinds(k), kinds(k_next)
         self_w = mix_ref[t]
         peer_w = 1.0 - self_w
         hid = a_ref[t].astype(jnp.float32)
@@ -97,7 +174,7 @@
             out = jnp.dot(act, q2[slot, l], preferred_element_type=jnp.float32)
             hid = (hid + out).astype(jnp.bfloat16).astype(jnp.float32)
             if l == 0:
-                send(t, n_chunks - 1).start()
+                start_send(t, k, shift, kind_now[n_chunks - 1], n_chunks - 1)
         d_hid = (2.0 / (rows * feat)) * (hid - t_ref[t].astype(jnp.float32))
         for l in reversed(range(n_layers)):
             d_out = d_hid.astype(jnp.bfloat16)
@@ -114,13 +191,29 @@
             w1[l] = self_w * w1[l] - rate * g1
 
         more = t < n_steps - 1
+        roles = pass_roles(k, shift, kind_now)
+
+        def pass_on(c):
+            if roles[c] is None:
+                return
+            role, to = roles[c]
+
+            @pl.when(role == 1)
+            def _():
+                pass_in(t, c).wait_recv()
+                pass_copy(t, c, to).start()
+
+        for c in range(min(RELAY_AHEAD, n_chunks)):
+            pass_on(c)
         for c in range(n_chunks):
             l, m = c // 2, c % 2
-            send(t, c).wait_recv()
+            if c + RELAY_AHEAD < n_chunks:
+                pass_on(c + RELAY_AHEAD)
+            wait_arrived(t, c)
 
             @pl.when(t > 0)
             def _():
-                send(t - 1, c).wait_send()
+                wait_sent(t - 1, c)
 
             if m == 0:
                 new = w1[l] + peer_w * r1[t, l].astype(jnp.float32)
@@ -130,17 +223,43 @@
                 new = w2[l] + peer_w * r2[t, l].astype(jnp.float32)
                 w2[l] = new
                 q2[nxt, l] = new.astype(jnp.bfloat16)
+            if c == 1:
+                for i, (cls, at, other) in enumerate(GATES):
+                    @pl.when((core == cls) & (t + 1 == at))
+                    def _():
+                        pl.semaphore_wait(gate_sem.at[i], 1)
             if c > 0:
                 @pl.when(more)
                 def _():
-                    send(t + 1, c - 1).start()
-        return carry
-
-    lax.fori_loop(0, n_steps, step, 0)
+                    start_send(t + 1, k_next, shift_next, kind_next[c - 1], c - 1)
+        for i, (cls, at, other) in enumerate(GATES):
+            @pl.when((core == 1 - cls) & (t == other))
+            def _():
+                pl.semaphore_signal(gate_sem.at[i], inc=1, device_id=as_id(me + 1 - 2 * core + n_dev), device_id_type=MESH)
+        left = []
+        for c in range(n_chunks):
+            if roles[c] is None:
+                continue
+
+            @pl.when(passed[len(left)] == 1)
+            def _():
+                pass_copy(t - 1, c, me + 1).wait_send()
+
+            left.append(roles[c][0])
+        return tuple(left)
+
+    n_pass = sum(1 for c in range(n_chunks) if any(row[c] for rows_ in ROUTES for row in rows_.values()))
+    passed = lax.fori_loop(0, n_steps, step, (jnp.int32(0),) * n_pass)
+    i = 0
     for c in range(n_chunks):
         load_out(c).start()
     for c in range(n_chunks):
-        send(n_steps - 1, c).wait_send()
+        if any(row[c] for rows_ in ROUTES for row in rows_.values()):
+            @pl.when(passed[i] == 1)
+            def _():
+                pass_copy(n_steps - 1, c, me + 1).wait_send()
+            i += 1
+        wait_sent(n_steps - 1, c)
         load_out(c).wait()
 
 
@@ -163,13 +282,15 @@
                 pltpu.VMEM((n_layers, feat, wide), f32), pltpu.VMEM((n_layers, wide, feat), f32),
                 pltpu.VMEM((2, n_layers, feat, wide), bf), pltpu.VMEM((2, n_layers, wide, feat), bf),
                 pltpu.VMEM((n_steps, n_layers, feat, wide), bf), pltpu.VMEM((n_steps, n_layers, wide, feat), bf),
+                pltpu.VMEM((n_steps, n_layers, feat, wide), bf), pltpu.VMEM((n_steps, n_layers, wide, feat), bf),
                 pltpu.VMEM((n_layers, rows, feat), bf), pltpu.VMEM((n_layers, rows, wide), bf),
                 pltpu.VMEM((n_layers, rows, wide), f32), pltpu.VMEM((n_layers, rows, feat), f32),
                 pltpu.VMEM((n_layers, rows, feat), f32),
                 pltpu.SemaphoreType.DMA((2 * n_layers + 2,)), pltpu.SemaphoreType.DMA((2, 2 * n_layers)),
-                pltpu.SemaphoreType.DMA((n_steps, 2 * n_layers)),
+                pltpu.SemaphoreType.DMA((n_steps, 2 * n_layers)), pltpu.SemaphoreType.DMA((2, 2 * n_layers)),
+                pltpu.SemaphoreType.DMA((n_steps, 2 * n_layers)), pltpu.SemaphoreType.REGULAR((len(GATES),)),
             ],
-            compiler_params=pltpu.CompilerParams(collective_id=0, has_side_effects=True, vmem_limit_bytes=48 * 1024 * 1024),
+            compiler_params=pltpu.CompilerParams(collective_id=0, has_side_effects=True, vmem_limit_bytes=63 * 1024 * 1024),
             name="gossip_run",
         )(mix_self[0, 0], inputs[0, 0], targets[0, 0], w_one[0, 0], w_two[0, 0])
         return out_one[None, None], out_two[None, None]

time: 514 us -> 438 us (0.85)
  the two profiles are of different devices: /device:TPU:63 before, /device:TPU:97 now
where the time goes in v2:
time: 438 us
  Pallas kernels  434 us (99%)
    pallas_call x1, Pallas kernels, device_run(): pl.pallas_call(lambda *refs: run_kernel(n_dev, n_inner, *refs), out_shape...  434 us

profile of v2, /device:TPU:97, one launch (start us, length us, event | category | flops | bytes accessed | tf_op | source)
XLA Modules:
  0.0 438.0 jit_solution(5011706827530396656)
XLA Ops:
  0.6 434.0 %gossip_run.1 = (f32[4,128,512]{2,1,0:T(8,128)}, f32[4,512,128]{2,1,0:T(8,128)}) custom-call(f32[16]{0:T(128)} %bitcast.13, bf16[16,64,128]{2,1,0:T(8,128)(2,1)} %bitcast.11, bf16[16,64,128]{2,1,0:T(8,128)(2,1)} %bitcast.12, f32[4,128,512]{2,1,0:T(8,128)} %bitcast.7, f32[4,512,128]{2,1,0:T(8,128)} %bitcast.8), custom_call_target="tpu_custom_call" | custom-call | tf_op jit(solution)/shard_map/gossip_run/pallas_call | solution.py:275
  434.7 0.0 copy-start
  434.7 2.4 copy.9
  437.0 0.0 copy-done
  437.0 1.0 copy.10
Async XLA Ops:
  434.7 2.4 copy-start

commit v3 on v2

--- a/solution.py
+++ b/solution.py
@@ -12,10 +12,10 @@
 GELU_B = 0.7978845608028654 * 0.044715
 
 ROUTES = (
-    {2: (2,) * 8, 4: (0, 1) * 4, 6: (0, 0, 0, 3) * 2, 7: (3,) * 8},
-    {1: (1,) * 8, 2: (0, 1) * 4, 3: (0, 1, 0, 0) * 2, 4: (1, 0) * 4},
+    {1: (0, 0, 0, 0, 1, 0, 0, 0), 2: (0, 4, 0, 0, 4, 0, 4, 0), 3: (1, 0, 1, 0, 1, 1, 0, 1), 6: (0, 0, 0, 3, 0, 0, 0, 3), 7: (3, 3, 3, 0, 3, 3, 3, 3)},
+    {1: (4, 4, 1, 0, 4, 4, 4, 4), 2: (2, 4, 2, 4, 2, 4, 2, 4), 3: (1, 0, 1, 0, 1, 1, 0, 1), 4: (0, 1, 0, 0, 0, 1, 0, 1)},
 )
-GATES = ((1, 1, 2), (1, 3, 4), (1, 5, 6), (1, 9, 10), (1, 11, 12), (1, 13, 14))
+GATES = ((1, 1, 2), (1, 3, 4), (1, 4, 6), (1, 5, 5), (1, 7, 7), (1, 9, 10), (1, 11, 11), (1, 12, 13), (1, 13, 12))
 RELAY_AHEAD = 5
 
 
@@ -57,7 +57,8 @@
     in_t.start()
 
     offsets = sorted({2 ** k for k in range(log_g)} | {2 ** k - 32 + n_dev for k in range(1, 5)}
-                     | {2 ** k - 8 + n_dev for k in range(1, 3)} | {n_dev - 96, n_dev - 64})
+                     | {2 ** k - 8 + n_dev for k in range(1, 3)} | {n_dev - 96, n_dev - 64} | {n_dev - 24}
+                     | {2 ** k - 8 + 32 for k in range(1, 3)})
     barrier = pltpu.get_barrier_semaphore()
     for off in offsets:
         pl.semaphore_signal(barrier, inc=1, device_id=as_id(me + n_dev - off), device_id_type=MESH)
@@ -87,8 +88,10 @@
         via_plane = (kind == 1) & (plane_pos + shift >= 32)
         via_line = (kind == 2) & (line_pos + shift >= 8)
         via_back = kind == 3
-        via = via_plane | via_line | via_back
+        via_row = (kind == 4) & (line_pos + shift >= 8)
+        via = via_plane | via_line | via_back | via_row
         stop = jnp.where(via_plane, me + shift - 32, jnp.where(via_line, me + shift - 8, me - jnp.where(k == 6, 96, 64)))
+        stop = jnp.where(via_row, me - plane_pos + (plane_pos + 8) % 32, stop)
 
         @pl.when(via)
         def _():
@@ -127,8 +130,10 @@
             plane = (kind == 1) & (plane_pos < shift)
             line = (kind == 2) & (line_pos < shift)
             back = kind == 3
+            row = (kind == 4) & (line_pos + shift >= 8)
             to = me + jnp.where(plane, 32, jnp.where(line, 8, n_dev - jnp.where(k == 6, 96, 64)))
-            out.append((jnp.where(plane | line | back, 1, 0), to))
+            to = jnp.where(row, me + shift - 8 + jnp.where(plane_pos < 8, 32, 0), to)
+            out.append((jnp.where(plane | line | back | row, 1, 0), to))
         return out
 
     for c in range(n_chunks):

time: 438 us -> 419 us (0.957)
  the two profiles are of different devices: /device:TPU:97 before, /device:TPU:69 now
where the time goes in v3:
time: 419 us
  Pallas kernels  415 us (99%)
    pallas_call x1, Pallas kernels, device_run(): pl.pallas_call(lambda *refs: run_kernel(n_dev, n_inner, *refs), out_shape...  415 us

profile of v3, /device:TPU:69, one launch (start us, length us, event | category | flops | bytes accessed | tf_op | source)
XLA Modules:
  0.0 418.9 jit_solution(4830893675595556831)
XLA Ops:
  0.6 415.0 %gossip_run.1 = (f32[4,128,512]{2,1,0:T(8,128)}, f32[4,512,128]{2,1,0:T(8,128)}) custom-call(f32[16]{0:T(128)} %bitcast.13, bf16[16,64,128]{2,1,0:T(8,128)(2,1)} %bitcast.11, bf16[16,64,128]{2,1,0:T(8,128)(2,1)} %bitcast.12, f32[4,128,512]{2,1,0:T(8,128)} %bitcast.7, f32[4,512,128]{2,1,0:T(8,128)} %bitcast.8), custom_call_target="tpu_custom_call" | custom-call | tf_op jit(solution)/shard_map/gossip_run/pallas_call | solution.py:280
  415.6 0.0 copy-start
  415.6 2.4 copy.9
  418.0 0.0 copy-done
  418.0 1.0 copy.10
Async XLA Ops:
  415.6 2.4 copy-start

commit v4 on v3

--- a/solution.py
+++ b/solution.py
@@ -12,11 +12,11 @@
 GELU_B = 0.7978845608028654 * 0.044715
 
 ROUTES = (
-    {1: (0, 0, 0, 0, 1, 0, 0, 0), 2: (0, 4, 0, 0, 4, 0, 4, 0), 3: (1, 0, 1, 0, 1, 1, 0, 1), 6: (0, 0, 0, 3, 0, 0, 0, 3), 7: (3, 3, 3, 0, 3, 3, 3, 3)},
-    {1: (4, 4, 1, 0, 4, 4, 4, 4), 2: (2, 4, 2, 4, 2, 4, 2, 4), 3: (1, 0, 1, 0, 1, 1, 0, 1), 4: (0, 1, 0, 0, 0, 1, 0, 1)},
+    {1: (0, 4, 0, 0, 0, 0, 0, 0), 2: (4, 4, 4, 4, 4, 4, 4, 4), 3: (0, 0, 0, 0, 1, 0, 0, 0), 4: (1, 1, 1, 1, 1, 1, 1, 1), 9: (0, 4, 0, 0, 0, 0, 0, 0), 10: (4, 4, 4, 4, 4, 4, 4, 4), 11: (1, 1, 0, 0, 1, 0, 1, 0)},
+    {1: (0, 4, 0, 0, 0, 0, 0, 0), 2: (1, 1, 1, 1, 1, 1, 1, 1), 3: (0, 0, 0, 1, 1, 0, 0, 0), 4: (1, 1, 1, 1, 1, 1, 1, 1), 6: (0, 3, 0, 0, 0, 3, 0, 0), 7: (3, 3, 3, 3, 3, 3, 3, 3), 9: (0, 4, 0, 0, 0, 0, 0, 0), 10: (1, 1, 1, 1, 1, 1, 1, 1), 11: (0, 0, 0, 0, 1, 0, 0, 0), 14: (0, 3, 0, 0, 0, 3, 0, 0), 15: (3, 3, 3, 3, 3, 3, 0, 3)},
 )
-GATES = ((1, 1, 2), (1, 3, 4), (1, 4, 6), (1, 5, 5), (1, 7, 7), (1, 9, 10), (1, 11, 11), (1, 12, 13), (1, 13, 12))
-RELAY_AHEAD = 5
+GATES = ((0, 1, 2), (0, 2, 3), (0, 3, 4), (0, 7, 6), (0, 9, 10), (0, 10, 11), (0, 13, 12), (0, 15, 14))
+RELAY_AHEAD = 7
 
 
 def two_power(k):
@@ -63,11 +63,11 @@
     for off in offsets:
         pl.semaphore_signal(barrier, inc=1, device_id=as_id(me + n_dev - off), device_id_type=MESH)
 
-    def kinds(k):
+    def kinds(t):
         out = [0] * n_chunks
         for cls in range(2):
-            for step_k, row in ROUTES[cls].items():
-                here = jnp.where((k == step_k) & (core == cls), 1, 0)
+            for at, row in ROUTES[cls].items():
+                here = jnp.where((t == at) & (core == cls), 1, 0)
                 out = [o + v * here if v else o for o, v in zip(out, row)]
         return out
 
@@ -89,8 +89,10 @@
         via_line = (kind == 2) & (line_pos + shift >= 8)
         via_back = kind == 3
         via_row = (kind == 4) & (line_pos + shift >= 8)
-        via = via_plane | via_line | via_back | via_row
+        via_two = kind == 5
+        via = via_plane | via_line | via_back | via_row | via_two
         stop = jnp.where(via_plane, me + shift - 32, jnp.where(via_line, me + shift - 8, me - jnp.where(k == 6, 96, 64)))
+        stop = jnp.where(via_two, me + 64, stop)
         stop = jnp.where(via_row, me - plane_pos + (plane_pos + 8) % 32, stop)
 
         @pl.when(via)
@@ -132,8 +134,10 @@
             back = kind == 3
             row = (kind == 4) & (line_pos + shift >= 8)
             to = me + jnp.where(plane, 32, jnp.where(line, 8, n_dev - jnp.where(k == 6, 96, 64)))
+            two = kind == 5
+            to = jnp.where(two, me + 64, to)
             to = jnp.where(row, me + shift - 8 + jnp.where(plane_pos < 8, 32, 0), to)
-            out.append((jnp.where(plane | line | back | row, 1, 0), to))
+            out.append((jnp.where(plane | line | back | row | two, 1, 0), to))
         return out
 
     for c in range(n_chunks):
@@ -159,7 +163,7 @@
         k = t % log_g
         k_next = (t + 1) % log_g
         shift, shift_next = two_power(k), two_power(k_next)
-        kind_now, kind_next = kinds(k), kinds(k_next)
+        kind_now, kind_next = kinds(t), kinds(t + 1)
         self_w = mix_ref[t]
         peer_w = 1.0 - self_w
         hid = a_ref[t].astype(jnp.float32)
@@ -237,6 +241,10 @@
                 @pl.when(more)
                 def _():
                     start_send(t + 1, k_next, shift_next, kind_next[c - 1], c - 1)
+
+                @pl.when(jnp.logical_not(more))
+                def _():
+                    load_out(c - 1).start()
         for i, (cls, at, other) in enumerate(GATES):
             @pl.when((core == 1 - cls) & (t == other))
             def _():
@@ -256,8 +264,7 @@
     n_pass = sum(1 for c in range(n_chunks) if any(row[c] for rows_ in ROUTES for row in rows_.values()))
     passed = lax.fori_loop(0, n_steps, step, (jnp.int32(0),) * n_pass)
     i = 0
-    for c in range(n_chunks):
-        load_out(c).start()
+    load_out(n_chunks - 1).start()
     for c in range(n_chunks):
         if any(row[c] for rows_ in ROUTES for row in rows_.values()):
             @pl.when(passed[i] == 1)
@@ -280,7 +287,7 @@
         out_one, out_two = pl.pallas_call(
             lambda *refs: run_kernel(n_dev, n_inner, *refs),
             out_shape=(jax.ShapeDtypeStruct((n_layers, feat, wide), f32), jax.ShapeDtypeStruct((n_layers, wide, feat), f32)),
-            in_specs=[pl.BlockSpec(memory_space=pltpu.SMEM)] + [pl.BlockSpec(memory_space=pl.ANY)] * 4,
+            in_specs=[pl.BlockSpec(memory_space=pltpu.SMEM)] + [pl.BlockSpec(memory_space=pltpu.HBM)] * 4,
             out_specs=(pl.BlockSpec(memory_space=pl.ANY),) * 2,
             scratch_shapes=[
                 pltpu.VMEM((n_steps, rows, feat), bf), pltpu.VMEM((n_steps, rows, feat), bf),
@@ -295,7 +302,7 @@
                 pltpu.SemaphoreType.DMA((n_steps, 2 * n_layers)), pltpu.SemaphoreType.DMA((2, 2 * n_layers)),
                 pltpu.SemaphoreType.DMA((n_steps, 2 * n_layers)), pltpu.SemaphoreType.REGULAR((len(GATES),)),
             ],
-            compiler_params=pltpu.CompilerParams(collective_id=0, has_side_effects=True, vmem_limit_bytes=63 * 1024 * 1024),
+            compiler_params=pltpu.CompilerParams(collective_id=0, has_side_effects=True, vmem_limit_bytes=60 * 1024 * 1024),
             name="gossip_run",
         )(mix_self[0, 0], inputs[0, 0], targets[0, 0], w_one[0, 0], w_two[0, 0])
         return out_one[None, None], out_two[None, None]

time: 419 us -> 390 us (0.931)
  the two profiles are of different devices: /device:TPU:69 before, /device:TPU:120 now
where the time goes in v4:
time: 390 us
  Pallas kernels  386 us (99%)
    pallas_call x1, Pallas kernels, device_run(): pl.pallas_call(lambda *refs: run_kernel(n_dev, n_inner, *refs), out_shape...  386 us

profile of v4, /device:TPU:120, one launch (start us, length us, event | category | flops | bytes accessed | tf_op | source)
XLA Modules:
  0.0 389.6 jit_solution(12753076015850238860)
XLA Ops:
  0.6 385.7 %gossip_run.1 = (f32[4,128,512]{2,1,0:T(8,128)}, f32[4,512,128]{2,1,0:T(8,128)}) custom-call(f32[16]{0:T(128)} %bitcast.13, bf16[16,64,128]{2,1,0:T(8,128)(2,1)} %bitcast.11, bf16[16,64,128]{2,1,0:T(8,128)(2,1)} %bitcast.12, f32[4,128,512]{2,1,0:T(8,128)} %bitcast.7, f32[4,512,128]{2,1,0:T(8,128)} %bitcast.8), custom_call_target="tpu_custom_call" | custom-call | tf_op jit(solution)/shard_map/gossip_run/pallas_call | solution.py:287
  386.3 0.0 copy-start
  386.3 2.4 copy.9
  388.7 0.0 copy-done
  388.7 1.0 copy.10
Async XLA Ops:
  386.3 2.4 copy-start
